TPU v7x, 32 devices: a whole 2x2x4 slice. The times are simulated.
32 devices in a mesh: row: 8 (over z, core), col: 4 (over y, x).
Axes of the slice: x: 2, y: 2, z: 4, core: 2. Of those that a mesh axis runs over, the one named last changes fastest.
Arguments:
- ladder_ints: float32 [4928, 4928], P('row', 'col'), may hold values from -0.078125 to 0.078125
- amplitudes: float32 [4928, 1024], P('row', 'col'), may hold values from -6 to 6
- phase_map: int32 [8], replicated, may hold values from 0 to 7, each once
Outputs:
- ladder_term: float32 [4928, 1024], P('row', 'col')
Inputs may be any that keep to these rules, and one draw needn't show every extreme that they name: `phase_map`: each phase appears once.
All inputs are finite; a program needn't handle non-finite values.
Results may differ from a plain program's by a relative error of at most 0.000078.
Values sent between devices are 32-bit elements; how exact they have to be, the bound alone decides.
No kernel may reach another device: no remote copies, remote signals or barrier semaphores. Data moves between devices by JAX's collectives and lax.ppermute only.
A program may use at most 320 MiB of HBM per device.

v0:
```python
import jax
import jax.numpy as jnp
from jax import lax
from jax.sharding import PartitionSpec as P


def per_device(ladder_ints, amplitudes, phase_map):
    phases = lax.axis_size("row")
    spread = lax.all_to_all(amplitudes, "col", split_axis=0, concat_axis=1, tiled=True)
    rows_each = spread.shape[0]
    piece = lax.all_gather(spread, "row", axis=0, tiled=True)
    count = piece.shape[0]
    position = jnp.arange(count, dtype=jnp.int32)
    source = position // rows_each
    within = position % rows_each
    columns = within * phases + jnp.take(phase_map, source)
    chosen = jnp.take(ladder_ints, columns, axis=1)
    partial_value = jnp.dot(
        chosen, piece, precision=lax.Precision.HIGHEST, preferred_element_type=jnp.float32
    )
    return lax.psum_scatter(partial_value, "col", scatter_dimension=1, tiled=True)


def solution(mesh):
    in_specs = (P("row", "col"), P("row", "col"), P())
    out_specs = P("row", "col")
    return jax.shard_map(
        per_device, mesh=mesh, in_specs=in_specs, out_specs=out_specs, check_vma=False
    )
```

profile of v0, /device:TPU:0, one launch (start us, length us, event | category | flops | bytes accessed | tf_op | source)
XLA Modules:
  0.0 142.9 jit_solution(8082048879229056640)
XLA Ops:
  6.5 0.0 all-gather.3.cloned.1.call-start
  6.5 1.2 all_to_all.14
  7.7 14.9 %all_to_all.19 = f32[4,154,256]{2,1,0:T(8,128)S(1)} all-to-all(f32[4,154,256]{2,1,0:T(8,128)S(1)} %all_to_all.14), channel_id=1, replica_groups=mesh['row'=8,'col'=4] {'col'}, dimensions={0} | all-to-all | bytes 1261568 | tf_op jit(solution)/shard_map/all_to_all | solution.py:9
  22.6 0.4 copy.8
  23.0 1.2 reshape.145
  24.2 0.0 all-gather.3.cloned.1.call-update
  24.2 0.0 copy-start.1
  24.2 0.0 reduce-scatter.2.cloned.1.call-start
  24.3 3.4 %copy.7 = f32[616,1232]{0,1:T(8,128)S(1)} copy(f32[616,1232]{1,0:T(8,128)} %param.3) | data formatting | bytes 6071296 | tf_op args[0]
  27.7 0.1 compare_reduce_fusion
  27.8 0.0 copy-done.1
  27.8 0.7 fusion.16
  28.5 4.4 %fusion.13 = s32[1232]{0:T(1024)S(1)} fusion(s32[]{:T(128)} %bitcast.1, s32[]{:T(128)} %bitcast.2, s32[]{:T(128)} %bitcast.3, s32[]{:T(128)} %bitcast.4, s32[]{:T(128)} %bitcast.5, s32[]{:T(128)} %bitcast.7, s32[]{:T(128)} %bitcast.6), kind=kLoop, calls=%fused_computation.38 | loop fusion | flops 28336 | bytes 4956 | tf_op jit(solution)/shard_map/jit(_take)/gather | solution.py:16
  32.9 0.7 compare_and_fusion
  33.5 0.1 fusion.14
  33.6 4.8 %gather_fusion = f32[1232,616]{1,0:T(8,128)} fusion(f32[616,1232]{0,1:T(8,128)S(1)} %copy.7, s32[2048]{0:T(1024)S(1)} %pad_clamp_fusion), kind=kCustom, calls=%fused_computation | custom fusion | bytes 6076224 | tf_op jit(solution)/shard_map/jit(_take)/gather | solution.py:17
  38.4 0.0 copy-start
  38.4 41.6 %all-gather.3.cloned.1.call-done = f32[8,154,1024]{2,1,0:T(8,128)} async-done(((f32[1,154,1024]{2,1,0:T(8,128)}), f32[8,154,1024]{2,1,0:T(8,128)}) %all-gather.3.cloned.1.call-update) | async-done | bytes 5046288 | tf_op jit(solution)/shard_map/all_gather | solution.py:11
  80.1 4.4 %reshape.146 = f32[1232,1024]{1,0:T(8,128)} reshape(f32[8,154,1024]{2,1,0:T(8,128)} %all-gather.3.cloned.1.call-done) | data formatting | bytes 10092544
  84.4 0.0 copy-done
  84.4 13.9 %fusion = f32[616,1024]{1,0:T(8,128)} fusion(f32[1232,1024]{1,0:T(8,128)} %reshape.146, f32[1232,616]{1,0:T(8,128)S(1)} %copy-done, pred[1232]{0:T(1024)(128)(4,1)S(1)} %get-tuple-element.5), kind=kOutput, calls=%fused_computation.1 | convolution fusion | flops 9326269440 | bytes 10606288 | tf_op jit(solution)/shard_map/dot_general | solution.py:18
  98.4 0.0 reduce-scatter.2.cloned.1.call-update
  98.4 37.7 %reduce-scatter.2.cloned.1.call-done = f32[616,256]{1,0:T(8,128)} async-done(((f32[616,1024]{1,0:T(8,128)}), f32[616,256]{1,0:T(8,128)}) %reduce-scatter.2.cloned.1.call-update) | async-done | bytes 630800 | tf_op jit(solution)/shard_map/reduce_scatter | solution.py:21
  (1 shorter events, 0.0 us)
Async XLA Ops:
  6.5 73.5 %all-gather.3.cloned.1.call-start = ((), (), s32[]{:S(2)}) async-start(), calls=%async_computation.3 | async-start | bytes 5898240 | tf_op jit(solution)/shard_map/all_gather | solution.py:11
  24.2 3.5 %copy-start.1 = (s32[8]{0:T(128)S(1)}, s32[8]{0:T(128)}, u32[]{:S(2)}) copy-start(s32[8]{0:T(128)} %param.5) | copy-start | bytes 100
  24.2 111.8 %reduce-scatter.2.cloned.1.call-start = ((), (), s32[]{:S(2)}) async-start(), calls=%async_computation.2 | async-start | bytes 3153920 | tf_op jit(solution)/shard_map/reduce_scatter | solution.py:21
  38.4 46.0 %copy-start = (f32[1232,616]{1,0:T(8,128)S(1)}, f32[1232,616]{1,0:T(8,128)}, u32[]{:S(2)}) copy-start(f32[1232,616]{1,0:T(8,128)} %gather_fusion) | copy-start | bytes 9106948
Sparse Core Ops, SparseCore 0:
  24.3 55.6 all-gather.2
  98.5 37.4 reduce-scatter.1
where the time goes:
time: 143 us
  waiting for transfers between devices  79.3 us (55%)
  local copies, waits for them, and re-layouts  16 us (11%)
  blocking collectives  14.9 us (10%)
  matrix products  13.9 us (10%)
  between operations  13.5 us (9%)
  other arithmetic  5.18 us (4%)
    all_gather x1, waiting for transfers between devices, per_device(): piece = lax.all_gather(spread, 'row', axis=0, tiled=True)  41.6 us
    reduce_scatter x1, waiting for transfers between devices, per_device(): lax.psum_scatter(partial_value, 'col', scatter_dimension=1, tiled=True)  37.7 us
    all_to_all x1, blocking collectives, per_device(): lax.all_to_all(amplitudes, 'col', split_axis=0, concat_axis=1, tiled=True)  14.9 us
    dot_general x1, matrix products, per_device(): jnp.dot(chosen, piece, precision=lax.Precision.HIGHEST, preferred_element...  13.9 us
    unnamed x7, local copies, waits for them, and re-layouts  8.95 us
    gather x1, local copies, waits for them, and re-layouts, per_device(): chosen = jnp.take(ladder_ints, columns, axis=1)  4.83 us
    gather x2, other arithmetic, per_device(): columns = within * phases + jnp.take(phase_map, source)  4.45 us
  transfers between devices with their start and end apart: 2, of which 2 were waited for; matrix products, arithmetic and copies ran while one was open for 10% of the time, Pallas kernels for 0%

commit v1 on v0

v1 whole, which is shorter than its diff:
```python
import functools

import jax
import jax.numpy as jnp
from jax import lax
from jax.experimental import pallas as pl
from jax.experimental.pallas import tpu as pltpu
from jax.sharding import PartitionSpec as P

TILE = 256


def ring_row(position, n):
    return jnp.where(position < n // 2, 2 * position, 2 * (n - 1 - position) + 1)


def ring_place(row, n):
    return jnp.where(row % 2 == 0, row // 2, n - 1 - row // 2)


def ring_pairs(n):
    order = list(range(0, n, 2)) + list(range(n - 1, 0, -2))
    forward = [(order[i], order[(i + 1) % n]) for i in range(n)]
    return forward, [(b, a) for a, b in forward]


def split(x):
    high = x.astype(jnp.bfloat16)
    low = (x - high.astype(jnp.float32)).astype(jnp.bfloat16)
    return high, low


def cut_kernel(cols, rows, source, *pieces):
    me = lax.axis_index("col")
    for piece in pieces:
        piece[rows:, :] = jnp.zeros((piece.shape[0] - rows, piece.shape[1]), jnp.float32)
    for own in range(cols):

        @pl.when(me == own)
        def _():
            for j, piece in enumerate(pieces):
                start = (own ^ j) * rows
                piece[:rows, :] = source[start : start + rows, :]


def cut(amplitudes, cols, rows, padded):
    width = amplitudes.shape[1]
    out = jax.ShapeDtypeStruct((padded, width), jnp.float32)
    return pl.pallas_call(
        functools.partial(cut_kernel, cols, rows),
        out_shape=[out] * cols,
        name="cut",
        cost_estimate=pl.CostEstimate(
            flops=amplitudes.size, bytes_accessed=8 * amplitudes.size, transcendentals=0
        ),
    )(amplitudes)


def order_kernel(phases, tiles, ints, high_out, low_out):
    group = TILE // phases
    into = lax.broadcasted_iota(jnp.int32, (TILE, TILE), 1)
    source = lax.broadcasted_iota(jnp.int32, (TILE, TILE), 0)
    wanted = (into % group) * phases + into // group
    pick = jnp.where(source == wanted, 1.0, 0.0).astype(jnp.bfloat16)
    total = ints.shape[1]
    for t in range(tiles):
        stop = min(TILE, total - t * TILE)
        high, low = split(ints[:, t * TILE : t * TILE + stop])
        chosen = pick[:stop, :]
        at = pl.ds(t * TILE, TILE)
        high_out[:, at] = jnp.dot(
            high, chosen, preferred_element_type=jnp.float32
        ).astype(jnp.bfloat16)
        low_out[:, at] = jnp.dot(
            low, chosen, preferred_element_type=jnp.float32
        ).astype(jnp.bfloat16)


def order(ints, phases, tiles):
    out = jax.ShapeDtypeStruct((ints.shape[0], tiles * TILE), jnp.bfloat16)
    return pl.pallas_call(
        functools.partial(order_kernel, phases, tiles),
        out_shape=[out, out],
        name="order",
        cost_estimate=pl.CostEstimate(
            flops=4 * ints.size * TILE, bytes_accessed=8 * ints.size, transcendentals=0
        ),
    )(ints)


def product_kernel(offsets, tiles, n_add, outs, phase_map, high, low, *refs):
    blocks = refs[: len(offsets)]
    adds = refs[len(offsets) : len(offsets) + len(n_add)]
    results = refs[len(offsets) + len(n_add) : len(offsets) + len(n_add) + len(outs)]
    t_high, t_low = refs[-2:]
    n = len(offsets)
    group = TILE // n
    place = ring_place(lax.axis_index("row"), n)
    for block, offset in zip(blocks, offsets):
        phase = phase_map[ring_row((place + offset + n) % n, n)]
        b_high, b_low = split(block[...])
        for t in range(tiles):
            at = pl.ds(pl.multiple_of(t * TILE + phase * group, group), group)
            t_high[at, :] = b_high[t * group : (t + 1) * group, :]
            t_low[at, :] = b_low[t * group : (t + 1) * group, :]
    total = jnp.dot(high[...], t_high[...], preferred_element_type=jnp.float32)
    total += jnp.dot(low[...], t_high[...], preferred_element_type=jnp.float32)
    total += jnp.dot(high[...], t_low[...], preferred_element_type=jnp.float32)
    parts = {}
    for result, (start, width) in zip(results, outs):
        value = total[:, start : start + width]
        for add, (first, size) in zip(adds, n_add):
            if first == start and size == width:
                value += add[...]
            elif start <= first and first + size <= start + width:
                parts.setdefault((start, width), []).append((add, first - start, size))
        result[...] = value
        for add, first, size in parts.get((start, width), []):
            result[:, first : first + size] += add[...]


def product(phase_map, high, low, blocks, offsets, tiles, adds, outs):
    rows, depth = high.shape
    width = blocks[0].shape[1]
    vmem = pl.BlockSpec(memory_space=pltpu.VMEM)
    spots = tuple((first, a.shape[1]) for a, first in adds)
    return pl.pallas_call(
        functools.partial(product_kernel, offsets, tiles, spots, outs),
        out_shape=[jax.ShapeDtypeStruct((rows, w), jnp.float32) for _, w in outs],
        in_specs=[pl.BlockSpec(memory_space=pltpu.SMEM)] + [vmem] * (2 + len(blocks) + len(adds)),
        scratch_shapes=[pltpu.VMEM((depth, width), jnp.bfloat16)] * 2,
        name="product",
        cost_estimate=pl.CostEstimate(
            flops=6 * rows * depth * width,
            bytes_accessed=4 * rows * depth + 4 * depth * width + 4 * rows * width,
            transcendentals=0,
        ),
    )(phase_map, high, low, *blocks, *[a for a, _ in adds])


def gather(chunk, n):
    forward, backward = ring_pairs(n)
    half = n // 2
    up, down = chunk, chunk
    found = [(0, chunk)]
    odd = {}
    for step in range(1, half):
        up = lax.ppermute(up, "row", forward)
        down = lax.ppermute(down, "row", backward)
        found += [(-step, up), (step, down)]
        if step % 2:
            odd[-step], odd[step] = up, down
    place = ring_place(lax.axis_index("row"), n)
    wanted = (half - 2 * place - 1 + half - 1 + 4 * n) % n - (half - 1)
    send = odd[1]
    for distance, block in odd.items():
        if distance != 1:
            send = jnp.where(wanted == distance, block, send)
    other = lax.ppermute(send, "row", [(i, i ^ 1) for i in range(n)])
    return found + [(half, other)]


def per_device(ladder_ints, amplitudes, phase_map):
    n = lax.axis_size("row")
    cols = lax.axis_size("col")
    rows = amplitudes.shape[0] // cols
    width = amplitudes.shape[1]
    group = TILE // n
    tiles = -(-rows // group)
    padded = tiles * group
    half = width // 2

    def partner(j):
        return [(i, i ^ j) for i in range(cols)]

    pieces = cut(amplitudes, cols, rows, padded)
    high, low = order(ladder_ints, n, tiles)

    def swap(x, j):
        return lax.ppermute(x, "col", partner(j))

    ranks = sorted(range(1, cols), key=lambda j: (-bin(j).count("1"), j))
    arrived = {j: swap(pieces[j], j) for j in ranks}

    far = [j for j in ranks if bin(j).count("1") > 1]
    near = [j for j in ranks if bin(j).count("1") == 1]
    chunks = [[(j, 0), (j, 1)] for j in far]
    for a in range(0, len(near), 2):
        pair = near[a : a + 2]
        if len(pair) == 2:
            chunks += [[(pair[0], h), (pair[1], h)] for h in (0, 1)]
        else:
            chunks += [[(pair[0], 0), (pair[0], 1)]]
    waiting = {(j, h): [] for j in range(cols) for h in (0, 1)}

    def multiply(chunk, adds, outs):
        found = gather(chunk, n)
        offsets = tuple(d for d, _ in found)
        return product(
            phase_map, high, low, [b for _, b in found], offsets, tiles, adds, outs
        )

    for chunk in chunks:
        if chunk[0][0] == chunk[1][0]:
            block = arrived[chunk[0][0]]
        else:
            block = jnp.concatenate(
                [arrived[j][:, h * half : (h + 1) * half] for j, h in chunk], axis=1
            )
        adds = [(a, i * half) for i, key in enumerate(chunk) for a in waiting[key]]
        sums = multiply(block, adds, ((0, half), (half, half)))
        for (j, h), value in zip(chunk, sums):
            bits = [1 << b for b in range(cols) if j >> b & 1]
            bit = bits[0] if h == 0 else bits[-1]
            waiting[j ^ bit, h].append(swap(value, bit))

    adds = [(a, h * half) for h in (0, 1) for a in waiting[0, h]]
    return multiply(pieces[0], adds, ((0, width),))[0]


def solution(mesh):
    in_specs = (P("row", "col"), P("row", "col"), P())
    out_specs = P("row", "col")
    return jax.shard_map(
        per_device, mesh=mesh, in_specs=in_specs, out_specs=out_specs, check_vma=False
    )
```

time: 143 us -> 96.1 us (0.67)
  waiting for transfers between devices: 79.3 us -> 29 us
  starting transfers between devices: 0.04 us -> 37.1 us
  Pallas kernels: 0 us -> 25.6 us
  blocking collectives: 14.9 us -> 0 us
  matrix products: 13.9 us -> 0 us
  between operations: 13.5 us -> 0.43 us
  local copies, waits for them, and re-layouts: 16 us -> 3.65 us
  other arithmetic: 5.18 us -> 0.19 us
    all_gather x1 -> x0, waiting for transfers between devices: 41.6 us -> none  [per_device(): piece = lax.all_gather(spread, 'row', axis=0, tiled=True)]
    reduce_scatter x1 -> x0, waiting for transfers between devices: 37.7 us -> none  [per_device(): lax.psum_scatter(partial_value, 'col', scatter_dimension=1, tiled=True)]
    ppermute x0 -> x37, starting transfers between devices: none -> 37.1 us  [the longest x12 24.8 us: gather(): up = lax.ppermute(up, 'row', forward)]
    ppermute x0 -> x37, waiting for transfers between devices: none -> 29 us  [the longest x9 11.6 us: swap(): return lax.ppermute(x, 'col', partner(j))]
    pallas_call x0 -> x6, Pallas kernels: none -> 25.6 us  [the longest x4 19.1 us: product(): pl.pallas_call(functools.partial(product_kernel, offsets, tiles, spots, o...]
    all_to_all x1 -> x0, blocking collectives: 14.9 us -> none  [per_device(): lax.all_to_all(amplitudes, 'col', split_axis=0, concat_axis=1, tiled=True)]
    dot_general x1 -> x0, matrix products: 13.9 us -> none  [per_device(): jnp.dot(chosen, piece, precision=lax.Precision.HIGHEST, preferred_element...]
    gather x2 -> x0, local copies, waits for them, and re-layouts: 5.51 us -> none  [the longest x1 4.83 us: per_device(): chosen = jnp.take(ladder_ints, columns, axis=1)]
  transfers between devices with their start and end apart: 2 -> 37, of which waited for: 2 -> 14; matrix products, arithmetic and copies ran while one was open for 10% -> 0% of each run, Pallas kernels for 0% -> 19%
where the time goes in v1:
time: 96.1 us; the launch traced here: 95.9 us
  starting transfers between devices  37.1 us (39%)
  waiting for transfers between devices  29 us (30%)
  Pallas kernels  25.6 us (27%)
  local copies, waits for them, and re-layouts  3.65 us (4%)
    ppermute x12, starting transfers between devices, gather(): up = lax.ppermute(up, 'row', forward)  24.8 us
    pallas_call x4, Pallas kernels, product(): pl.pallas_call(functools.partial(product_kernel, offsets, tiles, spots, o...  19.1 us
    ppermute x9, starting transfers between devices, swap(): return lax.ppermute(x, 'col', partner(j))  12 us
    ppermute x9, waiting for transfers between devices, swap(): return lax.ppermute(x, 'col', partner(j))  11.6 us
    ppermute x12, waiting for transfers between devices, gather(): up = lax.ppermute(up, 'row', forward)  8.22 us
    ppermute x12, waiting for transfers between devices, gather(): down = lax.ppermute(down, 'row', backward)  7.75 us
    pallas_call x1, Pallas kernels, order(): pl.pallas_call(functools.partial(order_kernel, phases, tiles), out_shape=...  4.55 us
    unnamed x76, local copies, waits for them, and re-layouts  3.63 us
  transfers between devices with their start and end apart: 37, of which 14 were waited for; matrix products, arithmetic and copies ran while one was open for 0% of the time, Pallas kernels for 19%

profile of v1, /device:TPU:0, one launch (start us, length us, event | category | flops | bytes accessed | tf_op | source)
XLA Modules:
  0.0 95.9 jit_solution(11899209987712743487)
XLA Ops:
  0.0 1.9 %cut.1 = (f32[160,256]{1,0:T(8,128)}, f32[160,256]{1,0:T(8,128)}, f32[160,256]{1,0:T(8,128)}, f32[160,256]{1,0:T(8,128)}) custom-call(f32[616,256]{1,0:T(8,128)} %source.1), custom_call_target="tpu_custom_call" | custom-call | flops 157696 | bytes 1261568 | tf_op jit(solution)/shard_map/cut/pallas_call | solution.py:49
  2.0 3.9 %collective-permute-start.16 = (f32[160,256]{1,0:T(8,128)}, f32[160,256]{1,0:T(8,128)S(1)}, u32[]{:S(2)}, u32[]{:S(2)}) collective-permute-start(f32[160,256]{1,0:T(8,128)} %get-tuple-element.22), channel_id=1, source_target_pairs={{0,3},{1,2},{2,1},{3,0},{4,7},{5,6},{6,5},{7,4},{8,11},{9,10},{10,... | collective-permute-start | bytes 491528 | tf_op jit(solution)/shard_map/ppermute | solution.py:180
  6.5 4.6 %collective-permute-done.16.refs_0_ = f32[160,256]{1,0:T(8,128)S(1)} collective-permute-done((f32[160,256]{1,0:T(8,128)}, f32[160,256]{1,0:T(8,128)S(1)}, u32[]{:S(2)}, u32[]{:S(2)}) %collective-permute-start.16) | collective-permute-done | bytes 163872 | tf_op jit(solution)/shard_map/ppermute | solution.py:180
  11.1 2.1 %collective-permute-start.17 = (f32[160,256]{1,0:T(8,128)S(1)}, f32[160,256]{1,0:T(8,128)S(1)}, u32[]{:S(2)}, u32[]{:S(2)}) collective-permute-start(f32[160,256]{1,0:T(8,128)S(1)} %collective-permute-done.16.refs_0_), channel_id=1, source_target_pairs={{0,8},{8,16},{16,24},{24,28},{28,20},{20,12},{12,4},{4,0},{1,9},{9... | collective-permute-start | bytes 491528 | tf_op jit(solution)/shard_map/ppermute | solution.py:148
  14.1 1.9 %collective-permute-done.17.refs_1_ = f32[160,256]{1,0:T(8,128)S(1)} collective-permute-done((f32[160,256]{1,0:T(8,128)S(1)}, f32[160,256]{1,0:T(8,128)S(1)}, u32[]{:S(2)}, u32[]{:S(2)}) %collective-permute-start.17) | collective-permute-done | bytes 163872 | tf_op jit(solution)/shard_map/ppermute | solution.py:148
  16.0 2.5 %collective-permute-start.19 = (f32[160,256]{1,0:T(8,128)S(1)}, f32[160,256]{1,0:T(8,128)S(1)}, u32[]{:S(2)}, u32[]{:S(2)}) collective-permute-start(f32[160,256]{1,0:T(8,128)S(1)} %collective-permute-done.17.refs_1_), channel_id=1, source_target_pairs={{0,8},{8,16},{16,24},{24,28},{28,20},{20,12},{12,4},{4,0},{1,9},{9... | collective-permute-start | bytes 491528 | tf_op jit(solution)/shard_map/ppermute | solution.py:148
  18.5 1.7 %collective-permute-done.18.refs_2_ = f32[160,256]{1,0:T(8,128)S(1)} collective-permute-done((f32[160,256]{1,0:T(8,128)S(1)}, f32[160,256]{1,0:T(8,128)S(1)}, u32[]{:S(2)}, u32[]{:S(2)}) %collective-permute-start.18) | collective-permute-done | bytes 163872 | tf_op jit(solution)/shard_map/ppermute | solution.py:149
  20.3 2.0 %collective-permute-start.27 = (f32[160,256]{1,0:T(8,128)S(1)}, f32[160,256]{1,0:T(8,128)S(1)}, u32[]{:S(2)}, u32[]{:S(2)}) collective-permute-start(f32[160,256]{1,0:T(8,128)S(1)} %pad_maximum_fusion.1.refs_0_), channel_id=1, source_target_pairs={{0,8},{8,16},{16,24},{24,28},{28,20},{20,12},{12,4},{4,0},{1,9},{9... | collective-permute-start | bytes 491528 | tf_op jit(solution)/shard_map/ppermute | solution.py:148
  22.4 2.0 %collective-permute-start.21 = (f32[160,256]{1,0:T(8,128)S(1)}, f32[160,256]{1,0:T(8,128)S(1)}, u32[]{:S(2)}, u32[]{:S(2)}) collective-permute-start(f32[160,256]{1,0:T(8,128)S(1)} %collective-permute-done.19.refs_3_), channel_id=1, source_target_pairs={{0,8},{8,16},{16,24},{24,28},{28,20},{20,12},{12,4},{4,0},{1,9},{9... | collective-permute-start | bytes 491528 | tf_op jit(solution)/shard_map/ppermute | solution.py:148
  24.4 2.9 %collective-permute-done.20.refs_4_ = f32[160,256]{1,0:T(8,128)S(1)} collective-permute-done((f32[160,256]{1,0:T(8,128)S(1)}, f32[160,256]{1,0:T(8,128)S(1)}, u32[]{:S(2)}, u32[]{:S(2)}) %collective-permute-start.20) | collective-permute-done | bytes 163872 | tf_op jit(solution)/shard_map/ppermute | solution.py:149
  27.3 2.0 %collective-permute-start = (f32[160,256]{1,0:T(8,128)}, f32[160,256]{1,0:T(8,128)S(1)}, u32[]{:S(2)}, u32[]{:S(2)}) collective-permute-start(f32[160,256]{1,0:T(8,128)} %get-tuple-element.19.refs_0_), channel_id=1, source_target_pairs={{0,8},{8,16},{16,24},{24,28},{28,20},{20,12},{12,4},{4,0},{1,9},{9... | collective-permute-start | bytes 491528 | tf_op jit(solution)/shard_map/ppermute | solution.py:148
  29.4 1.2 %collective-permute-start.9 = (f32[160,256]{1,0:T(8,128)S(1)}, f32[160,256]{1,0:T(8,128)S(1)}, u32[]{:S(2)}, u32[]{:S(2)}) collective-permute-start(f32[160,256]{1,0:T(8,128)S(1)} %pad_maximum_fusion.refs_0_), channel_id=1, source_target_pairs={{0,8},{8,16},{16,24},{24,28},{28,20},{20,12},{12,4},{4,0},{1,9},{9... | collective-permute-start | bytes 491528 | tf_op jit(solution)/shard_map/ppermute | solution.py:148
  30.7 2.0 %collective-permute-start.29 = (f32[160,256]{1,0:T(8,128)S(1)}, f32[160,256]{1,0:T(8,128)S(1)}, u32[]{:S(2)}, u32[]{:S(2)}) collective-permute-start(f32[160,256]{1,0:T(8,128)S(1)} %collective-permute-done.27.refs_1_), channel_id=1, source_target_pairs={{0,8},{8,16},{16,24},{24,28},{28,20},{20,12},{12,4},{4,0},{1,9},{9... | collective-permute-start | bytes 491528 | tf_op jit(solution)/shard_map/ppermute | solution.py:148
  32.7 1.7 %collective-permute-done.22.refs_6_ = f32[160,256]{1,0:T(8,128)S(1)} collective-permute-done((f32[160,256]{1,0:T(8,128)S(1)}, f32[160,256]{1,0:T(8,128)S(1)}, u32[]{:S(2)}, u32[]{:S(2)}) %collective-permute-start.22) | collective-permute-done | bytes 163872 | tf_op jit(solution)/shard_map/ppermute | solution.py:149
  34.6 2.8 %collective-permute-done.9.refs_1_ = f32[160,256]{1,0:T(8,128)S(1)} collective-permute-done((f32[160,256]{1,0:T(8,128)S(1)}, f32[160,256]{1,0:T(8,128)S(1)}, u32[]{:S(2)}, u32[]{:S(2)}) %collective-permute-start.9) | collective-permute-done | bytes 163872 | tf_op jit(solution)/shard_map/ppermute | solution.py:148
  37.5 2.4 %collective-permute-start.11 = (f32[160,256]{1,0:T(8,128)S(1)}, f32[160,256]{1,0:T(8,128)S(1)}, u32[]{:S(2)}, u32[]{:S(2)}) collective-permute-start(f32[160,256]{1,0:T(8,128)S(1)} %collective-permute-done.9.refs_1_), channel_id=1, source_target_pairs={{0,8},{8,16},{16,24},{24,28},{28,20},{20,12},{12,4},{4,0},{1,9},{9... | collective-permute-start | bytes 491528 | tf_op jit(solution)/shard_map/ppermute | solution.py:148
  40.9 2.5 %collective-permute-start.31 = (f32[160,256]{1,0:T(8,128)S(1)}, f32[160,256]{1,0:T(8,128)S(1)}, u32[]{:S(2)}, u32[]{:S(2)}) collective-permute-start(f32[160,256]{1,0:T(8,128)S(1)} %collective-permute-done.29.refs_3_), channel_id=1, source_target_pairs={{0,8},{8,16},{16,24},{24,28},{28,20},{20,12},{12,4},{4,0},{1,9},{9... | collective-permute-start | bytes 491528 | tf_op jit(solution)/shard_map/ppermute | solution.py:148
  44.1 4.6 %order.1 = (bf16[616,1280]{1,0:T(8,128)(2,1)}, bf16[616,1280]{1,0:T(8,128)(2,1)}) custom-call(f32[616,1232]{1,0:T(8,128)} %ints.1), custom_call_target="tpu_custom_call" | custom-call | flops 777125888 | bytes 6071296 | tf_op jit(solution)/shard_map/order/pallas_call | solution.py:81
  48.8 4.6 %product.4 = (f32[616,128]{1,0:T(8,128)}, f32[616,128]{1,0:T(8,128)}) custom-call(s32[8]{0:T(128)} %phase_map.7, bf16[616,1280]{1,0:T(8,128)(2,1)} %get-tuple-element.17.high, bf16[616,1280]{1,0:T(8,128)(2,1)} %get-tuple-element.18.low, f32[160,256]{1,0:T(8,128)} %copy-done.34, f32[160,256]{1,0:T(8,128)} %copy-done.30, f32[160,256]{1,0:T(8,128)} %copy-done.31, ...), custom_call_target="tpu_custom_call" | custom-call | flops 1211105280 | bytes 5095424 | tf_op jit(solution)/shard_map/product/pallas_call | solution.py:127
  53.4 2.0 %collective-permute-start.2 = (f32[160,256]{1,0:T(8,128)S(1)}, f32[160,256]{1,0:T(8,128)S(1)}, u32[]{:S(2)}, u32[]{:S(2)}) collective-permute-start(f32[160,256]{1,0:T(8,128)S(1)} %collective-permute-done.refs_1_), channel_id=1, source_target_pairs={{0,8},{8,16},{16,24},{24,28},{28,20},{20,12},{12,4},{4,0},{1,9},{9... | collective-permute-start | bytes 491528 | tf_op jit(solution)/shard_map/ppermute | solution.py:148
  55.5 2.0 %collective-permute-start.13 = (f32[160,256]{1,0:T(8,128)S(1)}, f32[160,256]{1,0:T(8,128)S(1)}, u32[]{:S(2)}, u32[]{:S(2)}) collective-permute-start(f32[160,256]{1,0:T(8,128)S(1)} %collective-permute-done.11.refs_3_), channel_id=1, source_target_pairs={{0,8},{8,16},{16,24},{24,28},{28,20},{20,12},{12,4},{4,0},{1,9},{9... | collective-permute-start | bytes 491528 | tf_op jit(solution)/shard_map/ppermute | solution.py:148
  57.5 1.6 %collective-permute-start.34 = (f32[616,128]{1,0:T(8,128)}, f32[616,128]{1,0:T(8,128)S(1)}, u32[]{:S(2)}, u32[]{:S(2)}) collective-permute-start(f32[616,128]{1,0:T(8,128)} %get-tuple-element.26), channel_id=1, source_target_pairs={{0,2},{1,3},{2,0},{3,1},{4,6},{5,7},{6,4},{7,5},{8,10},{9,11},{10,... | collective-permute-start | bytes 946184 | tf_op jit(solution)/shard_map/ppermute | solution.py:180
  59.2 2.5 %collective-permute-done.13.refs_5_ = f32[160,256]{1,0:T(8,128)S(1)} collective-permute-done((f32[160,256]{1,0:T(8,128)S(1)}, f32[160,256]{1,0:T(8,128)S(1)}, u32[]{:S(2)}, u32[]{:S(2)}) %collective-permute-start.13) | collective-permute-done | bytes 163872 | tf_op jit(solution)/shard_map/ppermute | solution.py:148
  62.8 1.5 %collective-permute-start.24 = (f32[616,128]{1,0:T(8,128)}, f32[616,128]{1,0:T(8,128)S(1)}, u32[]{:S(2)}, u32[]{:S(2)}) collective-permute-start(f32[616,128]{1,0:T(8,128)} %get-tuple-element.23), channel_id=1, source_target_pairs={{0,1},{1,0},{2,3},{3,2},{4,5},{5,4},{6,7},{7,6},{8,9},{9,8},{10,11... | collective-permute-start | bytes 946184 | tf_op jit(solution)/shard_map/ppermute | solution.py:180
  64.5 2.0 %collective-permute-start.4 = (f32[160,256]{1,0:T(8,128)S(1)}, f32[160,256]{1,0:T(8,128)S(1)}, u32[]{:S(2)}, u32[]{:S(2)}) collective-permute-start(f32[160,256]{1,0:T(8,128)S(1)} %collective-permute-done.2.refs_3_), channel_id=1, source_target_pairs={{0,8},{8,16},{16,24},{24,28},{28,20},{20,12},{12,4},{4,0},{1,9},{9... | collective-permute-start | bytes 491528 | tf_op jit(solution)/shard_map/ppermute | solution.py:148
  67.9 4.7 %product.6 = (f32[616,128]{1,0:T(8,128)}, f32[616,128]{1,0:T(8,128)}) custom-call(s32[8]{0:T(128)} %phase_map.7, bf16[616,1280]{1,0:T(8,128)(2,1)} %get-tuple-element.17.high, bf16[616,1280]{1,0:T(8,128)(2,1)} %get-tuple-element.18.low, f32[160,256]{1,0:T(8,128)} %copy-done, f32[160,256]{1,0:T(8,128)} %copy-done.3, f32[160,256]{1,0:T(8,128)} %copy-done.4, ...), custom_call_target="tpu_custom_call" | custom-call | flops 1211105280 | bytes 5095424 | tf_op jit(solution)/shard_map/product/pallas_call | solution.py:127
  73.3 1.6 %collective-permute-start.36 = (f32[616,128]{1,0:T(8,128)}, f32[616,128]{1,0:T(8,128)S(1)}, u32[]{:S(2)}, u32[]{:S(2)}) collective-permute-start(f32[616,128]{1,0:T(8,128)} %get-tuple-element.28), channel_id=1, source_target_pairs={{0,2},{1,3},{2,0},{3,1},{4,6},{5,7},{6,4},{7,5},{8,10},{9,11},{10,... | collective-permute-start | bytes 946184 | tf_op jit(solution)/shard_map/ppermute | solution.py:180
  75.6 4.7 %product.5 = (f32[616,128]{1,0:T(8,128)}, f32[616,128]{1,0:T(8,128)}) custom-call(s32[8]{0:T(128)} %phase_map.7, bf16[616,1280]{1,0:T(8,128)(2,1)} %get-tuple-element.17.high, bf16[616,1280]{1,0:T(8,128)(2,1)} %get-tuple-element.18.low, f32[160,256]{1,0:T(8,128)} %copy-done.1, f32[160,256]{1,0:T(8,128)} %copy-done.6, f32[160,256]{1,0:T(8,128)} %copy-done.7, ...), custom_call_target="tpu_custom_call" | custom-call | flops 1211105280 | bytes 5095424 | tf_op jit(solution)/shard_map/product/pallas_call | solution.py:127
  80.3 1.6 %collective-permute-start.25 = (f32[616,128]{1,0:T(8,128)}, f32[616,128]{1,0:T(8,128)S(1)}, u32[]{:S(2)}, u32[]{:S(2)}) collective-permute-start(f32[616,128]{1,0:T(8,128)} %get-tuple-element.24), channel_id=1, source_target_pairs={{0,1},{1,0},{2,3},{3,2},{4,5},{5,4},{6,7},{7,6},{8,9},{9,8},{10,11... | collective-permute-start | bytes 946184 | tf_op jit(solution)/shard_map/ppermute | solution.py:180
  82.7 1.4 %collective-permute-done.6.refs_7_ = f32[160,256]{1,0:T(8,128)S(1)} collective-permute-done((f32[160,256]{1,0:T(8,128)S(1)}, f32[160,256]{1,0:T(8,128)S(1)}, u32[]{:S(2)}, u32[]{:S(2)}) %collective-permute-start.6) | collective-permute-done | bytes 163872 | tf_op jit(solution)/shard_map/ppermute | solution.py:159
  84.1 4.8 %collective-permute-done.25.refs_8_ = f32[616,128]{1,0:T(8,128)S(1)} collective-permute-done((f32[616,128]{1,0:T(8,128)}, f32[616,128]{1,0:T(8,128)S(1)}, u32[]{:S(2)}, u32[]{:S(2)}) %collective-permute-start.25) | collective-permute-done | bytes 315424 | tf_op jit(solution)/shard_map/ppermute | solution.py:180
  90.9 5.0 %product.7 = f32[616,256]{1,0:T(8,128)} custom-call(s32[8]{0:T(128)} %phase_map.7, bf16[616,1280]{1,0:T(8,128)(2,1)} %get-tuple-element.17.high, bf16[616,1280]{1,0:T(8,128)(2,1)} %get-tuple-element.18.low, f32[160,256]{1,0:T(8,128)} %get-tuple-element.19.refs_0_, f32[160,256]{1,0:T(8,128)} %copy-done.2, f32[160,256]{1,0:T(8,128)} %copy-done.5, ...), custom_call_target="tpu_custom_call" | custom-call | flops 1211105280 | bytes 5095424 | tf_op jit(solution)/shard_map/product/pallas_call | solution.py:127
  (132 shorter events, 10.4 us)
Async XLA Ops:
  2.0 9.2 %collective-permute-start.16 = (f32[160,256]{1,0:T(8,128)}, f32[160,256]{1,0:T(8,128)S(1)}, u32[]{:S(2)}, u32[]{:S(2)}) collective-permute-start(f32[160,256]{1,0:T(8,128)} %get-tuple-element.22), channel_id=1, source_target_pairs={{0,3},{1,2},{2,1},{3,0},{4,7},{5,6},{6,5},{7,4},{8,11},{9,10},{10,... | collective-permute-start | bytes 491528 | tf_op jit(solution)/shard_map/ppermute | solution.py:180
  5.9 8.2 %collective-permute-start.7 = (f32[160,256]{1,0:T(8,128)}, f32[160,256]{1,0:T(8,128)S(1)}, u32[]{:S(2)}, u32[]{:S(2)}) collective-permute-start(f32[160,256]{1,0:T(8,128)} %get-tuple-element.20), channel_id=1, source_target_pairs={{0,1},{1,0},{2,3},{3,2},{4,5},{5,4},{6,7},{7,6},{8,9},{9,8},{10,11... | collective-permute-start | bytes 491528 | tf_op jit(solution)/shard_map/ppermute | solution.py:180
  6.4 13.9 %collective-permute-start.8 = (f32[160,256]{1,0:T(8,128)}, f32[160,256]{1,0:T(8,128)S(1)}, u32[]{:S(2)}, u32[]{:S(2)}) collective-permute-start(f32[160,256]{1,0:T(8,128)} %get-tuple-element.21), channel_id=1, source_target_pairs={{0,2},{1,3},{2,0},{3,1},{4,6},{5,7},{6,4},{7,5},{8,10},{9,11},{10,... | collective-permute-start | bytes 491528 | tf_op jit(solution)/shard_map/ppermute | solution.py:180
  13.2 7.1 %collective-permute-start.18 = (f32[160,256]{1,0:T(8,128)S(1)}, f32[160,256]{1,0:T(8,128)S(1)}, u32[]{:S(2)}, u32[]{:S(2)}) collective-permute-start(f32[160,256]{1,0:T(8,128)S(1)} %collective-permute-done.16.refs_0_), channel_id=1, source_target_pairs={{8,0},{16,8},{24,16},{28,24},{20,28},{12,20},{4,12},{0,4},{9,1},{1... | collective-permute-start | bytes 491528 | tf_op jit(solution)/shard_map/ppermute | solution.py:149
  16.0 6.3 %collective-permute-start.19 = (f32[160,256]{1,0:T(8,128)S(1)}, f32[160,256]{1,0:T(8,128)S(1)}, u32[]{:S(2)}, u32[]{:S(2)}) collective-permute-start(f32[160,256]{1,0:T(8,128)S(1)} %collective-permute-done.17.refs_1_), channel_id=1, source_target_pairs={{0,8},{8,16},{16,24},{24,28},{28,20},{20,12},{12,4},{4,0},{1,9},{9... | collective-permute-start | bytes 491528 | tf_op jit(solution)/shard_map/ppermute | solution.py:148
  20.3 7.1 %collective-permute-start.20 = (f32[160,256]{1,0:T(8,128)S(1)}, f32[160,256]{1,0:T(8,128)S(1)}, u32[]{:S(2)}, u32[]{:S(2)}) collective-permute-start(f32[160,256]{1,0:T(8,128)S(1)} %collective-permute-done.18.refs_2_), channel_id=1, source_target_pairs={{8,0},{16,8},{24,16},{28,24},{20,28},{12,20},{4,12},{0,4},{9,1},{1... | collective-permute-start | bytes 491528 | tf_op jit(solution)/shard_map/ppermute | solution.py:149
  20.3 9.1 %collective-permute-start.27 = (f32[160,256]{1,0:T(8,128)S(1)}, f32[160,256]{1,0:T(8,128)S(1)}, u32[]{:S(2)}, u32[]{:S(2)}) collective-permute-start(f32[160,256]{1,0:T(8,128)S(1)} %pad_maximum_fusion.1.refs_0_), channel_id=1, source_target_pairs={{0,8},{8,16},{16,24},{24,28},{28,20},{20,12},{12,4},{4,0},{1,9},{9... | collective-permute-start | bytes 491528 | tf_op jit(solution)/shard_map/ppermute | solution.py:148
  22.4 8.3 %collective-permute-start.28 = (f32[160,256]{1,0:T(8,128)S(1)}, f32[160,256]{1,0:T(8,128)S(1)}, u32[]{:S(2)}, u32[]{:S(2)}) collective-permute-start(f32[160,256]{1,0:T(8,128)S(1)} %pad_maximum_fusion.1.refs_0_), channel_id=1, source_target_pairs={{8,0},{16,8},{24,16},{28,24},{20,28},{12,20},{4,12},{0,4},{9,1},{1... | collective-permute-start | bytes 491528 | tf_op jit(solution)/shard_map/ppermute | solution.py:149
  22.4 8.3 %collective-permute-start.21 = (f32[160,256]{1,0:T(8,128)S(1)}, f32[160,256]{1,0:T(8,128)S(1)}, u32[]{:S(2)}, u32[]{:S(2)}) collective-permute-start(f32[160,256]{1,0:T(8,128)S(1)} %collective-permute-done.19.refs_3_), channel_id=1, source_target_pairs={{0,8},{8,16},{16,24},{24,28},{28,20},{20,12},{12,4},{4,0},{1,9},{9... | collective-permute-start | bytes 491528 | tf_op jit(solution)/shard_map/ppermute | solution.py:148
  27.3 7.1 %collective-permute-start.22 = (f32[160,256]{1,0:T(8,128)S(1)}, f32[160,256]{1,0:T(8,128)S(1)}, u32[]{:S(2)}, u32[]{:S(2)}) collective-permute-start(f32[160,256]{1,0:T(8,128)S(1)} %collective-permute-done.20.refs_4_), channel_id=1, source_target_pairs={{8,0},{16,8},{24,16},{28,24},{20,28},{12,20},{4,12},{0,4},{9,1},{1... | collective-permute-start | bytes 491528 | tf_op jit(solution)/shard_map/ppermute | solution.py:149
  27.3 7.1 %collective-permute-start = (f32[160,256]{1,0:T(8,128)}, f32[160,256]{1,0:T(8,128)S(1)}, u32[]{:S(2)}, u32[]{:S(2)}) collective-permute-start(f32[160,256]{1,0:T(8,128)} %get-tuple-element.19.refs_0_), channel_id=1, source_target_pairs={{0,8},{8,16},{16,24},{24,28},{28,20},{20,12},{12,4},{4,0},{1,9},{9... | collective-permute-start | bytes 491528 | tf_op jit(solution)/shard_map/ppermute | solution.py:148
  29.4 8.0 %collective-permute-start.9 = (f32[160,256]{1,0:T(8,128)S(1)}, f32[160,256]{1,0:T(8,128)S(1)}, u32[]{:S(2)}, u32[]{:S(2)}) collective-permute-start(f32[160,256]{1,0:T(8,128)S(1)} %pad_maximum_fusion.refs_0_), channel_id=1, source_target_pairs={{0,8},{8,16},{16,24},{24,28},{28,20},{20,12},{12,4},{4,0},{1,9},{9... | collective-permute-start | bytes 491528 | tf_op jit(solution)/shard_map/ppermute | solution.py:148
  30.6 6.9 %collective-permute-start.10 = (f32[160,256]{1,0:T(8,128)S(1)}, f32[160,256]{1,0:T(8,128)S(1)}, u32[]{:S(2)}, u32[]{:S(2)}) collective-permute-start(f32[160,256]{1,0:T(8,128)S(1)} %pad_maximum_fusion.refs_0_), channel_id=1, source_target_pairs={{8,0},{16,8},{24,16},{28,24},{20,28},{12,20},{4,12},{0,4},{9,1},{1... | collective-permute-start | bytes 491528 | tf_op jit(solution)/shard_map/ppermute | solution.py:149
  30.7 10.3 %collective-permute-start.29 = (f32[160,256]{1,0:T(8,128)S(1)}, f32[160,256]{1,0:T(8,128)S(1)}, u32[]{:S(2)}, u32[]{:S(2)}) collective-permute-start(f32[160,256]{1,0:T(8,128)S(1)} %collective-permute-done.27.refs_1_), channel_id=1, source_target_pairs={{0,8},{8,16},{16,24},{24,28},{28,20},{20,12},{12,4},{4,0},{1,9},{9... | collective-permute-start | bytes 491528 | tf_op jit(solution)/shard_map/ppermute | solution.py:148
  34.4 6.5 %collective-permute-start.30 = (f32[160,256]{1,0:T(8,128)S(1)}, f32[160,256]{1,0:T(8,128)S(1)}, u32[]{:S(2)}, u32[]{:S(2)}) collective-permute-start(f32[160,256]{1,0:T(8,128)S(1)} %collective-permute-done.28.refs_2_), channel_id=1, source_target_pairs={{8,0},{16,8},{24,16},{28,24},{20,28},{12,20},{4,12},{0,4},{9,1},{1... | collective-permute-start | bytes 491528 | tf_op jit(solution)/shard_map/ppermute | solution.py:149
  34.5 9.0 %collective-permute-start.23 = (f32[160,256]{1,0:T(8,128)S(1)}, f32[160,256]{1,0:T(8,128)S(1)}, u32[]{:S(2)}, u32[]{:S(2)}) collective-permute-start(f32[160,256]{1,0:T(8,128)S(1)} %select_select_fusion.1), channel_id=1, source_target_pairs={{0,4},{4,0},{8,12},{12,8},{16,20},{20,16},{24,28},{28,24},{1,5},{5... | collective-permute-start | bytes 491528 | tf_op jit(solution)/shard_map/ppermute | solution.py:159
  37.4 16.0 %collective-permute-start.1 = (f32[160,256]{1,0:T(8,128)S(1)}, f32[160,256]{1,0:T(8,128)S(1)}, u32[]{:S(2)}, u32[]{:S(2)}) collective-permute-start(f32[160,256]{1,0:T(8,128)S(1)} %copy-done.20), channel_id=1, source_target_pairs={{8,0},{16,8},{24,16},{28,24},{20,28},{12,20},{4,12},{0,4},{9,1},{1... | collective-permute-start | bytes 491528 | tf_op jit(solution)/shard_map/ppermute | solution.py:149
  37.5 17.9 %collective-permute-start.11 = (f32[160,256]{1,0:T(8,128)S(1)}, f32[160,256]{1,0:T(8,128)S(1)}, u32[]{:S(2)}, u32[]{:S(2)}) collective-permute-start(f32[160,256]{1,0:T(8,128)S(1)} %collective-permute-done.9.refs_1_), channel_id=1, source_target_pairs={{0,8},{8,16},{16,24},{24,28},{28,20},{20,12},{12,4},{4,0},{1,9},{9... | collective-permute-start | bytes 491528 | tf_op jit(solution)/shard_map/ppermute | solution.py:148
  40.9 14.5 %collective-permute-start.12 = (f32[160,256]{1,0:T(8,128)S(1)}, f32[160,256]{1,0:T(8,128)S(1)}, u32[]{:S(2)}, u32[]{:S(2)}) collective-permute-start(f32[160,256]{1,0:T(8,128)S(1)} %collective-permute-done.10.refs_2_), channel_id=1, source_target_pairs={{8,0},{16,8},{24,16},{28,24},{20,28},{12,20},{4,12},{0,4},{9,1},{1... | collective-permute-start | bytes 491528 | tf_op jit(solution)/shard_map/ppermute | solution.py:149
  40.9 16.5 %collective-permute-start.31 = (f32[160,256]{1,0:T(8,128)S(1)}, f32[160,256]{1,0:T(8,128)S(1)}, u32[]{:S(2)}, u32[]{:S(2)}) collective-permute-start(f32[160,256]{1,0:T(8,128)S(1)} %collective-permute-done.29.refs_3_), channel_id=1, source_target_pairs={{0,8},{8,16},{16,24},{24,28},{28,20},{20,12},{12,4},{4,0},{1,9},{9... | collective-permute-start | bytes 491528 | tf_op jit(solution)/shard_map/ppermute | solution.py:148
  44.1 13.4 %collective-permute-start.32 = (f32[160,256]{1,0:T(8,128)S(1)}, f32[160,256]{1,0:T(8,128)S(1)}, u32[]{:S(2)}, u32[]{:S(2)}) collective-permute-start(f32[160,256]{1,0:T(8,128)S(1)} %collective-permute-done.30.refs_4_), channel_id=1, source_target_pairs={{8,0},{16,8},{24,16},{28,24},{20,28},{12,20},{4,12},{0,4},{9,1},{1... | collective-permute-start | bytes 491528 | tf_op jit(solution)/shard_map/ppermute | solution.py:149
  53.4 11.0 %collective-permute-start.2 = (f32[160,256]{1,0:T(8,128)S(1)}, f32[160,256]{1,0:T(8,128)S(1)}, u32[]{:S(2)}, u32[]{:S(2)}) collective-permute-start(f32[160,256]{1,0:T(8,128)S(1)} %collective-permute-done.refs_1_), channel_id=1, source_target_pairs={{0,8},{8,16},{16,24},{24,28},{28,20},{20,12},{12,4},{4,0},{1,9},{9... | collective-permute-start | bytes 491528 | tf_op jit(solution)/shard_map/ppermute | solution.py:148
  55.4 9.0 %collective-permute-start.3 = (f32[160,256]{1,0:T(8,128)S(1)}, f32[160,256]{1,0:T(8,128)S(1)}, u32[]{:S(2)}, u32[]{:S(2)}) collective-permute-start(f32[160,256]{1,0:T(8,128)S(1)} %collective-permute-done.1.refs_2_), channel_id=1, source_target_pairs={{8,0},{16,8},{24,16},{28,24},{20,28},{12,20},{4,12},{0,4},{9,1},{1... | collective-permute-start | bytes 491528 | tf_op jit(solution)/shard_map/ppermute | solution.py:149
  57.5 9.0 %collective-permute-start.34 = (f32[616,128]{1,0:T(8,128)}, f32[616,128]{1,0:T(8,128)S(1)}, u32[]{:S(2)}, u32[]{:S(2)}) collective-permute-start(f32[616,128]{1,0:T(8,128)} %get-tuple-element.26), channel_id=1, source_target_pairs={{0,2},{1,3},{2,0},{3,1},{4,6},{5,7},{6,4},{7,5},{8,10},{9,11},{10,... | collective-permute-start | bytes 946184 | tf_op jit(solution)/shard_map/ppermute | solution.py:180
  62.8 12.0 %collective-permute-start.24 = (f32[616,128]{1,0:T(8,128)}, f32[616,128]{1,0:T(8,128)S(1)}, u32[]{:S(2)}, u32[]{:S(2)}) collective-permute-start(f32[616,128]{1,0:T(8,128)} %get-tuple-element.23), channel_id=1, source_target_pairs={{0,1},{1,0},{2,3},{3,2},{4,5},{5,4},{6,7},{7,6},{8,9},{9,8},{10,11... | collective-permute-start | bytes 946184 | tf_op jit(solution)/shard_map/ppermute | solution.py:180
  64.4 8.9 %collective-permute-start.15 = (f32[160,256]{1,0:T(8,128)S(1)}, f32[160,256]{1,0:T(8,128)S(1)}, u32[]{:S(2)}, u32[]{:S(2)}) collective-permute-start(f32[160,256]{1,0:T(8,128)S(1)} %select_select_fusion.2), channel_id=1, source_target_pairs={{0,4},{4,0},{8,12},{12,8},{16,20},{20,16},{24,28},{28,24},{1,5},{5... | collective-permute-start | bytes 491528 | tf_op jit(solution)/shard_map/ppermute | solution.py:159
  64.5 17.4 %collective-permute-start.4 = (f32[160,256]{1,0:T(8,128)S(1)}, f32[160,256]{1,0:T(8,128)S(1)}, u32[]{:S(2)}, u32[]{:S(2)}) collective-permute-start(f32[160,256]{1,0:T(8,128)S(1)} %collective-permute-done.2.refs_3_), channel_id=1, source_target_pairs={{0,8},{8,16},{16,24},{24,28},{28,20},{20,12},{12,4},{4,0},{1,9},{9... | collective-permute-start | bytes 491528 | tf_op jit(solution)/shard_map/ppermute | solution.py:148
  66.5 16.1 %collective-permute-start.5 = (f32[160,256]{1,0:T(8,128)S(1)}, f32[160,256]{1,0:T(8,128)S(1)}, u32[]{:S(2)}, u32[]{:S(2)}) collective-permute-start(f32[160,256]{1,0:T(8,128)S(1)} %collective-permute-done.3.refs_4_), channel_id=1, source_target_pairs={{8,0},{16,8},{24,16},{28,24},{20,28},{12,20},{4,12},{0,4},{9,1},{1... | collective-permute-start | bytes 491528 | tf_op jit(solution)/shard_map/ppermute | solution.py:149
  72.7 11.4 %collective-permute-start.35 = (f32[616,128]{1,0:T(8,128)}, f32[616,128]{1,0:T(8,128)S(1)}, u32[]{:S(2)}, u32[]{:S(2)}) collective-permute-start(f32[616,128]{1,0:T(8,128)} %get-tuple-element.27), channel_id=1, source_target_pairs={{0,1},{1,0},{2,3},{3,2},{4,5},{5,4},{6,7},{7,6},{8,9},{9,8},{10,11... | collective-permute-start | bytes 946184 | tf_op jit(solution)/shard_map/ppermute | solution.py:180
  73.3 10.8 %collective-permute-start.36 = (f32[616,128]{1,0:T(8,128)}, f32[616,128]{1,0:T(8,128)S(1)}, u32[]{:S(2)}, u32[]{:S(2)}) collective-permute-start(f32[616,128]{1,0:T(8,128)} %get-tuple-element.28), channel_id=1, source_target_pairs={{0,2},{1,3},{2,0},{3,1},{4,6},{5,7},{6,4},{7,5},{8,10},{9,11},{10,... | collective-permute-start | bytes 946184 | tf_op jit(solution)/shard_map/ppermute | solution.py:180
  80.3 8.6 %collective-permute-start.25 = (f32[616,128]{1,0:T(8,128)}, f32[616,128]{1,0:T(8,128)S(1)}, u32[]{:S(2)}, u32[]{:S(2)}) collective-permute-start(f32[616,128]{1,0:T(8,128)} %get-tuple-element.24), channel_id=1, source_target_pairs={{0,1},{1,0},{2,3},{3,2},{4,5},{5,4},{6,7},{7,6},{8,9},{9,8},{10,11... | collective-permute-start | bytes 946184 | tf_op jit(solution)/shard_map/ppermute | solution.py:180
  81.9 8.3 %collective-permute-start.26 = (f32[616,128]{1,0:T(8,128)}, f32[616,128]{1,0:T(8,128)S(1)}, u32[]{:S(2)}, u32[]{:S(2)}) collective-permute-start(f32[616,128]{1,0:T(8,128)} %get-tuple-element.25), channel_id=1, source_target_pairs={{0,2},{1,3},{2,0},{3,1},{4,6},{5,7},{6,4},{7,5},{8,10},{9,11},{10,... | collective-permute-start | bytes 946184 | tf_op jit(solution)/shard_map/ppermute | solution.py:180
  (43 other events, 609.1 us)

commit v2 on v1

--- a/solution.py
+++ b/solution.py
@@ -16,6 +16,11 @@
 
 def ring_place(row, n):
     return jnp.where(row % 2 == 0, row // 2, n - 1 - row // 2)
+
+
+def room(*arrays):
+    total = sum(a.size * a.dtype.itemsize for a in arrays)
+    return pltpu.CompilerParams(vmem_limit_bytes=total + total // 4 + (2 << 20))
 
 
 def ring_pairs(n):
@@ -50,6 +55,7 @@
         functools.partial(cut_kernel, cols, rows),
         out_shape=[out] * cols,
         name="cut",
+        compiler_params=room(amplitudes, *[out] * cols),
         cost_estimate=pl.CostEstimate(
             flops=amplitudes.size, bytes_accessed=8 * amplitudes.size, transcendentals=0
         ),
@@ -82,6 +88,7 @@
         functools.partial(order_kernel, phases, tiles),
         out_shape=[out, out],
         name="order",
+        compiler_params=room(ints, out, out),
         cost_estimate=pl.CostEstimate(
             flops=4 * ints.size * TILE, bytes_accessed=8 * ints.size, transcendentals=0
         ),
@@ -124,12 +131,15 @@
     width = blocks[0].shape[1]
     vmem = pl.BlockSpec(memory_space=pltpu.VMEM)
     spots = tuple((first, a.shape[1]) for a, first in adds)
+    results = [jax.ShapeDtypeStruct((rows, w), jnp.float32) for _, w in outs]
+    held = jax.ShapeDtypeStruct((depth, width), jnp.float32)
     return pl.pallas_call(
         functools.partial(product_kernel, offsets, tiles, spots, outs),
-        out_shape=[jax.ShapeDtypeStruct((rows, w), jnp.float32) for _, w in outs],
+        out_shape=results,
         in_specs=[pl.BlockSpec(memory_space=pltpu.SMEM)] + [vmem] * (2 + len(blocks) + len(adds)),
         scratch_shapes=[pltpu.VMEM((depth, width), jnp.bfloat16)] * 2,
         name="product",
+        compiler_params=room(high, low, *blocks, *[a for a, _ in adds], *results, held),
         cost_estimate=pl.CostEstimate(
             flops=6 * rows * depth * width,
             bytes_accessed=4 * rows * depth + 4 * depth * width + 4 * rows * width,

time: 96.1 us -> 82.8 us (0.86)
  Pallas kernels: 25.6 us -> 10.7 us
  starting transfers between devices: 37.1 us -> 39.3 us
    pallas_call x4, Pallas kernels: 19.1 us -> 9.6 us  [product(): pl.pallas_call(functools.partial(product_kernel, offsets, tiles, spots, o...]
    pallas_call x1, Pallas kernels: 4.55 us -> 1 us  [order(): pl.pallas_call(functools.partial(order_kernel, phases, tiles), out_shape=...]
    ppermute x9, starting transfers between devices: 12 us -> 13.9 us  [swap(): return lax.ppermute(x, 'col', partner(j))]
    pallas_call x1, Pallas kernels: 1.95 us -> 0.06 us  [cut(): pl.pallas_call(functools.partial(cut_kernel, cols, rows), out_shape=[out]...]
    unnamed x76 -> x6, local copies, waits for them, and re-layouts: 3.63 us -> 2.97 us
  transfers between devices with their start and end apart: 37 -> 37, of which waited for: 14 -> 15; matrix products, arithmetic and copies ran while one was open for 0% -> 0% of each run, Pallas kernels for 19% -> 9%
where the time goes in v2:
time: 82.8 us; the launch traced here: 82.6 us
  starting transfers between devices  39.3 us (47%)
  waiting for transfers between devices  29.3 us (35%)
  Pallas kernels  10.7 us (13%)
  local copies, waits for them, and re-layouts  3 us (4%)
    ppermute x12, starting transfers between devices, gather(): up = lax.ppermute(up, 'row', forward)  25.1 us
    ppermute x9, starting transfers between devices, swap(): return lax.ppermute(x, 'col', partner(j))  13.9 us
    ppermute x9, waiting for transfers between devices, swap(): return lax.ppermute(x, 'col', partner(j))  12 us
    pallas_call x4, Pallas kernels, product(): pl.pallas_call(functools.partial(product_kernel, offsets, tiles, spots, o...  9.6 us
    ppermute x12, waiting for transfers between devices, gather(): up = lax.ppermute(up, 'row', forward)  8.35 us
    ppermute x12, waiting for transfers between devices, gather(): down = lax.ppermute(down, 'row', backward)  7.47 us
    unnamed x6, local copies, waits for them, and re-layouts  2.97 us
  transfers between devices with their start and end apart: 37, of which 15 were waited for; matrix products, arithmetic and copies ran while one was open for 0% of the time, Pallas kernels for 9%

profile of v2, /device:TPU:0, one launch (start us, length us, event | category | flops | bytes accessed | tf_op | source)
XLA Modules:
  0.0 82.6 jit_solution(733802519884247803)
XLA Ops:
  1.1 4.0 %collective-permute-start.16 = (f32[160,256]{1,0:T(8,128)S(1)}, f32[160,256]{1,0:T(8,128)S(1)}, u32[]{:S(2)}, u32[]{:S(2)}) collective-permute-start(f32[160,256]{1,0:T(8,128)S(1)} %get-tuple-element.22), channel_id=1, source_target_pairs={{0,3},{1,2},{2,1},{3,0},{4,7},{5,6},{6,5},{7,4},{8,11},{9,10},{10,... | collective-permute-start | bytes 491528 | tf_op jit(solution)/shard_map/ppermute | solution.py:190
  5.8 4.4 %collective-permute-done.16.refs_0_ = f32[160,256]{1,0:T(8,128)S(1)} collective-permute-done((f32[160,256]{1,0:T(8,128)S(1)}, f32[160,256]{1,0:T(8,128)S(1)}, u32[]{:S(2)}, u32[]{:S(2)}) %collective-permute-start.16) | collective-permute-done | bytes 163872 | tf_op jit(solution)/shard_map/ppermute | solution.py:190
  10.2 2.1 %collective-permute-start.17 = (f32[160,256]{1,0:T(8,128)S(1)}, f32[160,256]{1,0:T(8,128)S(1)}, u32[]{:S(2)}, u32[]{:S(2)}) collective-permute-start(f32[160,256]{1,0:T(8,128)S(1)} %collective-permute-done.16.refs_0_), channel_id=1, source_target_pairs={{0,8},{8,16},{16,24},{24,28},{28,20},{20,12},{12,4},{4,0},{1,9},{9... | collective-permute-start | bytes 491528 | tf_op jit(solution)/shard_map/ppermute | solution.py:158
  13.1 1.9 %collective-permute-done.17.refs_1_ = f32[160,256]{1,0:T(8,128)S(1)} collective-permute-done((f32[160,256]{1,0:T(8,128)S(1)}, f32[160,256]{1,0:T(8,128)S(1)}, u32[]{:S(2)}, u32[]{:S(2)}) %collective-permute-start.17) | collective-permute-done | bytes 163872 | tf_op jit(solution)/shard_map/ppermute | solution.py:158
  15.1 2.5 %collective-permute-start.19 = (f32[160,256]{1,0:T(8,128)S(1)}, f32[160,256]{1,0:T(8,128)S(1)}, u32[]{:S(2)}, u32[]{:S(2)}) collective-permute-start(f32[160,256]{1,0:T(8,128)S(1)} %collective-permute-done.17.refs_1_), channel_id=1, source_target_pairs={{0,8},{8,16},{16,24},{24,28},{28,20},{20,12},{12,4},{4,0},{1,9},{9... | collective-permute-start | bytes 491528 | tf_op jit(solution)/shard_map/ppermute | solution.py:158
  17.6 1.8 %collective-permute-done.18.refs_2_ = f32[160,256]{1,0:T(8,128)S(1)} collective-permute-done((f32[160,256]{1,0:T(8,128)S(1)}, f32[160,256]{1,0:T(8,128)S(1)}, u32[]{:S(2)}, u32[]{:S(2)}) %collective-permute-start.18) | collective-permute-done | bytes 163872 | tf_op jit(solution)/shard_map/ppermute | solution.py:159
  19.4 2.0 %collective-permute-start.27 = (f32[160,256]{1,0:T(8,128)S(1)}, f32[160,256]{1,0:T(8,128)S(1)}, u32[]{:S(2)}, u32[]{:S(2)}) collective-permute-start(f32[160,256]{1,0:T(8,128)S(1)} %pad_maximum_fusion.1.refs_0_), channel_id=1, source_target_pairs={{0,8},{8,16},{16,24},{24,28},{28,20},{20,12},{12,4},{4,0},{1,9},{9... | collective-permute-start | bytes 491528 | tf_op jit(solution)/shard_map/ppermute | solution.py:158
  21.4 2.0 %collective-permute-start.21 = (f32[160,256]{1,0:T(8,128)S(1)}, f32[160,256]{1,0:T(8,128)S(1)}, u32[]{:S(2)}, u32[]{:S(2)}) collective-permute-start(f32[160,256]{1,0:T(8,128)S(1)} %collective-permute-done.19.refs_3_), channel_id=1, source_target_pairs={{0,8},{8,16},{16,24},{24,28},{28,20},{20,12},{12,4},{4,0},{1,9},{9... | collective-permute-start | bytes 491528 | tf_op jit(solution)/shard_map/ppermute | solution.py:158
  23.4 3.0 %collective-permute-done.20.refs_4_ = f32[160,256]{1,0:T(8,128)S(1)} collective-permute-done((f32[160,256]{1,0:T(8,128)S(1)}, f32[160,256]{1,0:T(8,128)S(1)}, u32[]{:S(2)}, u32[]{:S(2)}) %collective-permute-start.20) | collective-permute-done | bytes 163872 | tf_op jit(solution)/shard_map/ppermute | solution.py:159
  26.4 2.0 %collective-permute-start = (f32[160,256]{1,0:T(8,128)S(1)}, f32[160,256]{1,0:T(8,128)S(1)}, u32[]{:S(2)}, u32[]{:S(2)}) collective-permute-start(f32[160,256]{1,0:T(8,128)S(1)} %get-tuple-element.19.refs_0_), channel_id=1, source_target_pairs={{0,8},{8,16},{16,24},{24,28},{28,20},{20,12},{12,4},{4,0},{1,9},{9... | collective-permute-start | bytes 491528 | tf_op jit(solution)/shard_map/ppermute | solution.py:158
  28.4 1.5 %collective-permute-start.9 = (f32[160,256]{1,0:T(8,128)S(1)}, f32[160,256]{1,0:T(8,128)S(1)}, u32[]{:S(2)}, u32[]{:S(2)}) collective-permute-start(f32[160,256]{1,0:T(8,128)S(1)} %pad_maximum_fusion.refs_0_), channel_id=1, source_target_pairs={{0,8},{8,16},{16,24},{24,28},{28,20},{20,12},{12,4},{4,0},{1,9},{9... | collective-permute-start | bytes 491528 | tf_op jit(solution)/shard_map/ppermute | solution.py:158
  29.9 2.0 %collective-permute-start.29 = (f32[160,256]{1,0:T(8,128)S(1)}, f32[160,256]{1,0:T(8,128)S(1)}, u32[]{:S(2)}, u32[]{:S(2)}) collective-permute-start(f32[160,256]{1,0:T(8,128)S(1)} %collective-permute-done.27.refs_1_), channel_id=1, source_target_pairs={{0,8},{8,16},{16,24},{24,28},{28,20},{20,12},{12,4},{4,0},{1,9},{9... | collective-permute-start | bytes 491528 | tf_op jit(solution)/shard_map/ppermute | solution.py:158
  31.9 1.5 %collective-permute-done.22.refs_6_ = f32[160,256]{1,0:T(8,128)S(1)} collective-permute-done((f32[160,256]{1,0:T(8,128)S(1)}, f32[160,256]{1,0:T(8,128)S(1)}, u32[]{:S(2)}, u32[]{:S(2)}) %collective-permute-start.22) | collective-permute-done | bytes 163872 | tf_op jit(solution)/shard_map/ppermute | solution.py:159
  33.6 2.9 %collective-permute-done.9.refs_1_ = f32[160,256]{1,0:T(8,128)S(1)} collective-permute-done((f32[160,256]{1,0:T(8,128)S(1)}, f32[160,256]{1,0:T(8,128)S(1)}, u32[]{:S(2)}, u32[]{:S(2)}) %collective-permute-start.9) | collective-permute-done | bytes 163872 | tf_op jit(solution)/shard_map/ppermute | solution.py:158
  36.6 2.4 %collective-permute-start.11 = (f32[160,256]{1,0:T(8,128)S(1)}, f32[160,256]{1,0:T(8,128)S(1)}, u32[]{:S(2)}, u32[]{:S(2)}) collective-permute-start(f32[160,256]{1,0:T(8,128)S(1)} %collective-permute-done.9.refs_1_), channel_id=1, source_target_pairs={{0,8},{8,16},{16,24},{24,28},{28,20},{20,12},{12,4},{4,0},{1,9},{9... | collective-permute-start | bytes 491528 | tf_op jit(solution)/shard_map/ppermute | solution.py:158
  40.0 2.5 %collective-permute-start.31 = (f32[160,256]{1,0:T(8,128)S(1)}, f32[160,256]{1,0:T(8,128)S(1)}, u32[]{:S(2)}, u32[]{:S(2)}) collective-permute-start(f32[160,256]{1,0:T(8,128)S(1)} %collective-permute-done.29.refs_3_), channel_id=1, source_target_pairs={{0,8},{8,16},{16,24},{24,28},{28,20},{20,12},{12,4},{4,0},{1,9},{9... | collective-permute-start | bytes 491528 | tf_op jit(solution)/shard_map/ppermute | solution.py:158
  42.5 1.9 %copy-done = f32[616,1232]{1,0:T(8,128)S(1)} copy-done((f32[616,1232]{1,0:T(8,128)S(1)}, f32[616,1232]{1,0:T(8,128)}, u32[]{:S(2)}) %copy-start) | copy-done | bytes 3035672
  45.4 2.2 %product.4 = (f32[616,128]{1,0:T(8,128)S(1)}, f32[616,128]{1,0:T(8,128)S(1)}) custom-call(s32[8]{0:T(128)S(1)} %copy-done.2, bf16[616,1280]{1,0:T(8,128)(2,1)S(1)} %get-tuple-element.17.high, bf16[616,1280]{1,0:T(8,128)(2,1)S(1)} %get-tuple-element.18.low, f32[160,256]{1,0:T(8,128)S(1)} %collective-permute-done.16.refs_0_, ...), custom_call_target="tpu_custom_call" | custom-call | flops 1211105280 | bytes 5095424 | tf_op jit(solution)/shard_map/product/pallas_call | solution.py:136
  47.6 2.0 %collective-permute-start.2 = (f32[160,256]{1,0:T(8,128)S(1)}, f32[160,256]{1,0:T(8,128)S(1)}, u32[]{:S(2)}, u32[]{:S(2)}) collective-permute-start(f32[160,256]{1,0:T(8,128)S(1)} %collective-permute-done.refs_1_), channel_id=1, source_target_pairs={{0,8},{8,16},{16,24},{24,28},{28,20},{20,12},{12,4},{4,0},{1,9},{9... | collective-permute-start | bytes 491528 | tf_op jit(solution)/shard_map/ppermute | solution.py:158
  49.7 2.0 %collective-permute-start.13 = (f32[160,256]{1,0:T(8,128)S(1)}, f32[160,256]{1,0:T(8,128)S(1)}, u32[]{:S(2)}, u32[]{:S(2)}) collective-permute-start(f32[160,256]{1,0:T(8,128)S(1)} %collective-permute-done.11.refs_3_), channel_id=1, source_target_pairs={{0,8},{8,16},{16,24},{24,28},{28,20},{20,12},{12,4},{4,0},{1,9},{9... | collective-permute-start | bytes 491528 | tf_op jit(solution)/shard_map/ppermute | solution.py:158
  51.7 1.6 %collective-permute-start.34 = (f32[616,128]{1,0:T(8,128)S(1)}, f32[616,128]{1,0:T(8,128)S(1)}, u32[]{:S(2)}, u32[]{:S(2)}) collective-permute-start(f32[616,128]{1,0:T(8,128)S(1)} %get-tuple-element.26), channel_id=1, source_target_pairs={{0,2},{1,3},{2,0},{3,1},{4,6},{5,7},{6,4},{7,5},{8,10},{9,11},{10,... | collective-permute-start | bytes 946184 | tf_op jit(solution)/shard_map/ppermute | solution.py:190
  53.4 2.5 %collective-permute-done.13.refs_5_ = f32[160,256]{1,0:T(8,128)S(1)} collective-permute-done((f32[160,256]{1,0:T(8,128)S(1)}, f32[160,256]{1,0:T(8,128)S(1)}, u32[]{:S(2)}, u32[]{:S(2)}) %collective-permute-start.13) | collective-permute-done | bytes 163872 | tf_op jit(solution)/shard_map/ppermute | solution.py:158
  57.0 1.5 %collective-permute-start.24 = (f32[616,128]{1,0:T(8,128)S(1)}, f32[616,128]{1,0:T(8,128)S(1)}, u32[]{:S(2)}, u32[]{:S(2)}) collective-permute-start(f32[616,128]{1,0:T(8,128)S(1)} %get-tuple-element.23), channel_id=1, source_target_pairs={{0,1},{1,0},{2,3},{3,2},{4,5},{5,4},{6,7},{7,6},{8,9},{9,8},{10,11... | collective-permute-start | bytes 946184 | tf_op jit(solution)/shard_map/ppermute | solution.py:190
  58.7 2.0 %collective-permute-start.4 = (f32[160,256]{1,0:T(8,128)S(1)}, f32[160,256]{1,0:T(8,128)S(1)}, u32[]{:S(2)}, u32[]{:S(2)}) collective-permute-start(f32[160,256]{1,0:T(8,128)S(1)} %collective-permute-done.2.refs_3_), channel_id=1, source_target_pairs={{0,8},{8,16},{16,24},{24,28},{28,20},{20,12},{12,4},{4,0},{1,9},{9... | collective-permute-start | bytes 491528 | tf_op jit(solution)/shard_map/ppermute | solution.py:158
  60.7 2.2 %product.6 = (f32[616,128]{1,0:T(8,128)S(1)}, f32[616,128]{1,0:T(8,128)S(1)}) custom-call(s32[8]{0:T(128)S(1)} %copy-done.2, bf16[616,1280]{1,0:T(8,128)(2,1)S(1)} %get-tuple-element.17.high, bf16[616,1280]{1,0:T(8,128)(2,1)S(1)} %get-tuple-element.18.low, f32[160,256]{1,0:T(8,128)S(1)} %pad_maximum_fusion.1.refs_0_, ...), custom_call_target="tpu_custom_call" | custom-call | flops 1211105280 | bytes 5095424 | tf_op jit(solution)/shard_map/product/pallas_call | solution.py:136
  63.5 1.6 %collective-permute-start.36 = (f32[616,128]{1,0:T(8,128)S(1)}, f32[616,128]{1,0:T(8,128)S(1)}, u32[]{:S(2)}, u32[]{:S(2)}) collective-permute-start(f32[616,128]{1,0:T(8,128)S(1)} %get-tuple-element.28), channel_id=1, source_target_pairs={{0,2},{1,3},{2,0},{3,1},{4,6},{5,7},{6,4},{7,5},{8,10},{9,11},{10,... | collective-permute-start | bytes 946184 | tf_op jit(solution)/shard_map/ppermute | solution.py:190
  65.7 2.2 %product.5 = (f32[616,128]{1,0:T(8,128)S(1)}, f32[616,128]{1,0:T(8,128)S(1)}) custom-call(s32[8]{0:T(128)S(1)} %copy-done.2, bf16[616,1280]{1,0:T(8,128)(2,1)S(1)} %get-tuple-element.17.high, bf16[616,1280]{1,0:T(8,128)(2,1)S(1)} %get-tuple-element.18.low, f32[160,256]{1,0:T(8,128)S(1)} %pad_maximum_fusion.refs_0_, ...), custom_call_target="tpu_custom_call" | custom-call | flops 1211105280 | bytes 5095424 | tf_op jit(solution)/shard_map/product/pallas_call | solution.py:136
  67.9 2.5 %collective-permute-start.25 = (f32[616,128]{1,0:T(8,128)S(1)}, f32[616,128]{1,0:T(8,128)S(1)}, u32[]{:S(2)}, u32[]{:S(2)}) collective-permute-start(f32[616,128]{1,0:T(8,128)S(1)} %get-tuple-element.24), channel_id=1, source_target_pairs={{0,1},{1,0},{2,3},{3,2},{4,5},{5,4},{6,7},{7,6},{8,9},{9,8},{10,11... | collective-permute-start | bytes 946184 | tf_op jit(solution)/shard_map/ppermute | solution.py:190
  70.4 1.6 %collective-permute-start.26 = (f32[616,128]{1,0:T(8,128)S(1)}, f32[616,128]{1,0:T(8,128)S(1)}, u32[]{:S(2)}, u32[]{:S(2)}) collective-permute-start(f32[616,128]{1,0:T(8,128)S(1)} %get-tuple-element.25), channel_id=1, source_target_pairs={{0,2},{1,3},{2,0},{3,1},{4,6},{5,7},{6,4},{7,5},{8,10},{9,11},{10,... | collective-permute-start | bytes 946184 | tf_op jit(solution)/shard_map/ppermute | solution.py:190
  72.1 1.4 %collective-permute-done.6.refs_7_ = f32[160,256]{1,0:T(8,128)S(1)} collective-permute-done((f32[160,256]{1,0:T(8,128)S(1)}, f32[160,256]{1,0:T(8,128)S(1)}, u32[]{:S(2)}, u32[]{:S(2)}) %collective-permute-start.6) | collective-permute-done | bytes 163872 | tf_op jit(solution)/shard_map/ppermute | solution.py:169
  73.8 5.4 %collective-permute-done.25.refs_8_ = f32[616,128]{1,0:T(8,128)S(1)} collective-permute-done((f32[616,128]{1,0:T(8,128)S(1)}, f32[616,128]{1,0:T(8,128)S(1)}, u32[]{:S(2)}, u32[]{:S(2)}) %collective-permute-start.25) | collective-permute-done | bytes 315424 | tf_op jit(solution)/shard_map/ppermute | solution.py:190
  79.6 3.0 %product.7 = f32[616,256]{1,0:T(8,128)} custom-call(s32[8]{0:T(128)S(1)} %copy-done.2, bf16[616,1280]{1,0:T(8,128)(2,1)S(1)} %get-tuple-element.17.high, bf16[616,1280]{1,0:T(8,128)(2,1)S(1)} %get-tuple-element.18.low, f32[160,256]{1,0:T(8,128)S(1)} %get-tuple-element.19.refs_0_, f32[160,256]{1,0:T(8,128)S(1)} %collective-permute-done.refs_1_, ...), custom_call_target="tpu_custom_call" | custom-call | flops 1211105280 | bytes 5095424 | tf_op jit(solution)/shard_map/product/pallas_call | solution.py:136
  (62 shorter events, 8.3 us)
Async XLA Ops:
  1.1 9.0 %collective-permute-start.16 = (f32[160,256]{1,0:T(8,128)S(1)}, f32[160,256]{1,0:T(8,128)S(1)}, u32[]{:S(2)}, u32[]{:S(2)}) collective-permute-start(f32[160,256]{1,0:T(8,128)S(1)} %get-tuple-element.22), channel_id=1, source_target_pairs={{0,3},{1,2},{2,1},{3,0},{4,7},{5,6},{6,5},{7,4},{8,11},{9,10},{10,... | collective-permute-start | bytes 491528 | tf_op jit(solution)/shard_map/ppermute | solution.py:190
  5.1 8.0 %collective-permute-start.7 = (f32[160,256]{1,0:T(8,128)S(1)}, f32[160,256]{1,0:T(8,128)S(1)}, u32[]{:S(2)}, u32[]{:S(2)}) collective-permute-start(f32[160,256]{1,0:T(8,128)S(1)} %get-tuple-element.20), channel_id=1, source_target_pairs={{0,1},{1,0},{2,3},{3,2},{4,5},{5,4},{6,7},{7,6},{8,9},{9,8},{10,11... | collective-permute-start | bytes 491528 | tf_op jit(solution)/shard_map/ppermute | solution.py:190
  5.7 13.7 %collective-permute-start.8 = (f32[160,256]{1,0:T(8,128)S(1)}, f32[160,256]{1,0:T(8,128)S(1)}, u32[]{:S(2)}, u32[]{:S(2)}) collective-permute-start(f32[160,256]{1,0:T(8,128)S(1)} %get-tuple-element.21), channel_id=1, source_target_pairs={{0,2},{1,3},{2,0},{3,1},{4,6},{5,7},{6,4},{7,5},{8,10},{9,11},{10,... | collective-permute-start | bytes 491528 | tf_op jit(solution)/shard_map/ppermute | solution.py:190
  12.2 7.1 %collective-permute-start.18 = (f32[160,256]{1,0:T(8,128)S(1)}, f32[160,256]{1,0:T(8,128)S(1)}, u32[]{:S(2)}, u32[]{:S(2)}) collective-permute-start(f32[160,256]{1,0:T(8,128)S(1)} %collective-permute-done.16.refs_0_), channel_id=1, source_target_pairs={{8,0},{16,8},{24,16},{28,24},{20,28},{12,20},{4,12},{0,4},{9,1},{1... | collective-permute-start | bytes 491528 | tf_op jit(solution)/shard_map/ppermute | solution.py:159
  15.1 6.3 %collective-permute-start.19 = (f32[160,256]{1,0:T(8,128)S(1)}, f32[160,256]{1,0:T(8,128)S(1)}, u32[]{:S(2)}, u32[]{:S(2)}) collective-permute-start(f32[160,256]{1,0:T(8,128)S(1)} %collective-permute-done.17.refs_1_), channel_id=1, source_target_pairs={{0,8},{8,16},{16,24},{24,28},{28,20},{20,12},{12,4},{4,0},{1,9},{9... | collective-permute-start | bytes 491528 | tf_op jit(solution)/shard_map/ppermute | solution.py:158
  19.3 7.1 %collective-permute-start.20 = (f32[160,256]{1,0:T(8,128)S(1)}, f32[160,256]{1,0:T(8,128)S(1)}, u32[]{:S(2)}, u32[]{:S(2)}) collective-permute-start(f32[160,256]{1,0:T(8,128)S(1)} %collective-permute-done.18.refs_2_), channel_id=1, source_target_pairs={{8,0},{16,8},{24,16},{28,24},{20,28},{12,20},{4,12},{0,4},{9,1},{1... | collective-permute-start | bytes 491528 | tf_op jit(solution)/shard_map/ppermute | solution.py:159
  19.4 9.1 %collective-permute-start.27 = (f32[160,256]{1,0:T(8,128)S(1)}, f32[160,256]{1,0:T(8,128)S(1)}, u32[]{:S(2)}, u32[]{:S(2)}) collective-permute-start(f32[160,256]{1,0:T(8,128)S(1)} %pad_maximum_fusion.1.refs_0_), channel_id=1, source_target_pairs={{0,8},{8,16},{16,24},{24,28},{28,20},{20,12},{12,4},{4,0},{1,9},{9... | collective-permute-start | bytes 491528 | tf_op jit(solution)/shard_map/ppermute | solution.py:158
  21.4 8.5 %collective-permute-start.28 = (f32[160,256]{1,0:T(8,128)S(1)}, f32[160,256]{1,0:T(8,128)S(1)}, u32[]{:S(2)}, u32[]{:S(2)}) collective-permute-start(f32[160,256]{1,0:T(8,128)S(1)} %pad_maximum_fusion.1.refs_0_), channel_id=1, source_target_pairs={{8,0},{16,8},{24,16},{28,24},{20,28},{12,20},{4,12},{0,4},{9,1},{1... | collective-permute-start | bytes 491528 | tf_op jit(solution)/shard_map/ppermute | solution.py:159
  21.4 8.5 %collective-permute-start.21 = (f32[160,256]{1,0:T(8,128)S(1)}, f32[160,256]{1,0:T(8,128)S(1)}, u32[]{:S(2)}, u32[]{:S(2)}) collective-permute-start(f32[160,256]{1,0:T(8,128)S(1)} %collective-permute-done.19.refs_3_), channel_id=1, source_target_pairs={{0,8},{8,16},{16,24},{24,28},{28,20},{20,12},{12,4},{4,0},{1,9},{9... | collective-permute-start | bytes 491528 | tf_op jit(solution)/shard_map/ppermute | solution.py:158
  26.4 7.1 %collective-permute-start.22 = (f32[160,256]{1,0:T(8,128)S(1)}, f32[160,256]{1,0:T(8,128)S(1)}, u32[]{:S(2)}, u32[]{:S(2)}) collective-permute-start(f32[160,256]{1,0:T(8,128)S(1)} %collective-permute-done.20.refs_4_), channel_id=1, source_target_pairs={{8,0},{16,8},{24,16},{28,24},{20,28},{12,20},{4,12},{0,4},{9,1},{1... | collective-permute-start | bytes 491528 | tf_op jit(solution)/shard_map/ppermute | solution.py:159
  26.4 7.1 %collective-permute-start = (f32[160,256]{1,0:T(8,128)S(1)}, f32[160,256]{1,0:T(8,128)S(1)}, u32[]{:S(2)}, u32[]{:S(2)}) collective-permute-start(f32[160,256]{1,0:T(8,128)S(1)} %get-tuple-element.19.refs_0_), channel_id=1, source_target_pairs={{0,8},{8,16},{16,24},{24,28},{28,20},{20,12},{12,4},{4,0},{1,9},{9... | collective-permute-start | bytes 491528 | tf_op jit(solution)/shard_map/ppermute | solution.py:158
  28.4 8.1 %collective-permute-start.9 = (f32[160,256]{1,0:T(8,128)S(1)}, f32[160,256]{1,0:T(8,128)S(1)}, u32[]{:S(2)}, u32[]{:S(2)}) collective-permute-start(f32[160,256]{1,0:T(8,128)S(1)} %pad_maximum_fusion.refs_0_), channel_id=1, source_target_pairs={{0,8},{8,16},{16,24},{24,28},{28,20},{20,12},{12,4},{4,0},{1,9},{9... | collective-permute-start | bytes 491528 | tf_op jit(solution)/shard_map/ppermute | solution.py:158
  29.9 6.7 %collective-permute-start.10 = (f32[160,256]{1,0:T(8,128)S(1)}, f32[160,256]{1,0:T(8,128)S(1)}, u32[]{:S(2)}, u32[]{:S(2)}) collective-permute-start(f32[160,256]{1,0:T(8,128)S(1)} %pad_maximum_fusion.refs_0_), channel_id=1, source_target_pairs={{8,0},{16,8},{24,16},{28,24},{20,28},{12,20},{4,12},{0,4},{9,1},{1... | collective-permute-start | bytes 491528 | tf_op jit(solution)/shard_map/ppermute | solution.py:159
  29.9 10.1 %collective-permute-start.29 = (f32[160,256]{1,0:T(8,128)S(1)}, f32[160,256]{1,0:T(8,128)S(1)}, u32[]{:S(2)}, u32[]{:S(2)}) collective-permute-start(f32[160,256]{1,0:T(8,128)S(1)} %collective-permute-done.27.refs_1_), channel_id=1, source_target_pairs={{0,8},{8,16},{16,24},{24,28},{28,20},{20,12},{12,4},{4,0},{1,9},{9... | collective-permute-start | bytes 491528 | tf_op jit(solution)/shard_map/ppermute | solution.py:158
  33.5 6.6 %collective-permute-start.30 = (f32[160,256]{1,0:T(8,128)S(1)}, f32[160,256]{1,0:T(8,128)S(1)}, u32[]{:S(2)}, u32[]{:S(2)}) collective-permute-start(f32[160,256]{1,0:T(8,128)S(1)} %collective-permute-done.28.refs_2_), channel_id=1, source_target_pairs={{8,0},{16,8},{24,16},{28,24},{20,28},{12,20},{4,12},{0,4},{9,1},{1... | collective-permute-start | bytes 491528 | tf_op jit(solution)/shard_map/ppermute | solution.py:159
  33.5 9.0 %collective-permute-start.23 = (f32[160,256]{1,0:T(8,128)S(1)}, f32[160,256]{1,0:T(8,128)S(1)}, u32[]{:S(2)}, u32[]{:S(2)}) collective-permute-start(f32[160,256]{1,0:T(8,128)S(1)} %select_select_fusion.1), channel_id=1, source_target_pairs={{0,4},{4,0},{8,12},{12,8},{16,20},{20,16},{24,28},{28,24},{1,5},{5... | collective-permute-start | bytes 491528 | tf_op jit(solution)/shard_map/ppermute | solution.py:169
  36.5 11.1 %collective-permute-start.1 = (f32[160,256]{1,0:T(8,128)S(1)}, f32[160,256]{1,0:T(8,128)S(1)}, u32[]{:S(2)}, u32[]{:S(2)}) collective-permute-start(f32[160,256]{1,0:T(8,128)S(1)} %get-tuple-element.19.refs_0_), channel_id=1, source_target_pairs={{8,0},{16,8},{24,16},{28,24},{20,28},{12,20},{4,12},{0,4},{9,1},{1... | collective-permute-start | bytes 491528 | tf_op jit(solution)/shard_map/ppermute | solution.py:159
  36.6 13.1 %collective-permute-start.11 = (f32[160,256]{1,0:T(8,128)S(1)}, f32[160,256]{1,0:T(8,128)S(1)}, u32[]{:S(2)}, u32[]{:S(2)}) collective-permute-start(f32[160,256]{1,0:T(8,128)S(1)} %collective-permute-done.9.refs_1_), channel_id=1, source_target_pairs={{0,8},{8,16},{16,24},{24,28},{28,20},{20,12},{12,4},{4,0},{1,9},{9... | collective-permute-start | bytes 491528 | tf_op jit(solution)/shard_map/ppermute | solution.py:158
  40.0 9.6 %collective-permute-start.12 = (f32[160,256]{1,0:T(8,128)S(1)}, f32[160,256]{1,0:T(8,128)S(1)}, u32[]{:S(2)}, u32[]{:S(2)}) collective-permute-start(f32[160,256]{1,0:T(8,128)S(1)} %collective-permute-done.10.refs_2_), channel_id=1, source_target_pairs={{8,0},{16,8},{24,16},{28,24},{20,28},{12,20},{4,12},{0,4},{9,1},{1... | collective-permute-start | bytes 491528 | tf_op jit(solution)/shard_map/ppermute | solution.py:159
  40.0 11.7 %collective-permute-start.31 = (f32[160,256]{1,0:T(8,128)S(1)}, f32[160,256]{1,0:T(8,128)S(1)}, u32[]{:S(2)}, u32[]{:S(2)}) collective-permute-start(f32[160,256]{1,0:T(8,128)S(1)} %collective-permute-done.29.refs_3_), channel_id=1, source_target_pairs={{0,8},{8,16},{16,24},{24,28},{28,20},{20,12},{12,4},{4,0},{1,9},{9... | collective-permute-start | bytes 491528 | tf_op jit(solution)/shard_map/ppermute | solution.py:158
  42.5 9.2 %collective-permute-start.32 = (f32[160,256]{1,0:T(8,128)S(1)}, f32[160,256]{1,0:T(8,128)S(1)}, u32[]{:S(2)}, u32[]{:S(2)}) collective-permute-start(f32[160,256]{1,0:T(8,128)S(1)} %collective-permute-done.30.refs_4_), channel_id=1, source_target_pairs={{8,0},{16,8},{24,16},{28,24},{20,28},{12,20},{4,12},{0,4},{9,1},{1... | collective-permute-start | bytes 491528 | tf_op jit(solution)/shard_map/ppermute | solution.py:159
  47.6 10.9 %collective-permute-start.2 = (f32[160,256]{1,0:T(8,128)S(1)}, f32[160,256]{1,0:T(8,128)S(1)}, u32[]{:S(2)}, u32[]{:S(2)}) collective-permute-start(f32[160,256]{1,0:T(8,128)S(1)} %collective-permute-done.refs_1_), channel_id=1, source_target_pairs={{0,8},{8,16},{16,24},{24,28},{28,20},{20,12},{12,4},{4,0},{1,9},{9... | collective-permute-start | bytes 491528 | tf_op jit(solution)/shard_map/ppermute | solution.py:158
  49.7 9.0 %collective-permute-start.3 = (f32[160,256]{1,0:T(8,128)S(1)}, f32[160,256]{1,0:T(8,128)S(1)}, u32[]{:S(2)}, u32[]{:S(2)}) collective-permute-start(f32[160,256]{1,0:T(8,128)S(1)} %collective-permute-done.1.refs_2_), channel_id=1, source_target_pairs={{8,0},{16,8},{24,16},{28,24},{20,28},{12,20},{4,12},{0,4},{9,1},{1... | collective-permute-start | bytes 491528 | tf_op jit(solution)/shard_map/ppermute | solution.py:159
  49.7 6.2 %collective-permute-start.13 = (f32[160,256]{1,0:T(8,128)S(1)}, f32[160,256]{1,0:T(8,128)S(1)}, u32[]{:S(2)}, u32[]{:S(2)}) collective-permute-start(f32[160,256]{1,0:T(8,128)S(1)} %collective-permute-done.11.refs_3_), channel_id=1, source_target_pairs={{0,8},{8,16},{16,24},{24,28},{28,20},{20,12},{12,4},{4,0},{1,9},{9... | collective-permute-start | bytes 491528 | tf_op jit(solution)/shard_map/ppermute | solution.py:158
  51.7 9.0 %collective-permute-start.34 = (f32[616,128]{1,0:T(8,128)S(1)}, f32[616,128]{1,0:T(8,128)S(1)}, u32[]{:S(2)}, u32[]{:S(2)}) collective-permute-start(f32[616,128]{1,0:T(8,128)S(1)} %get-tuple-element.26), channel_id=1, source_target_pairs={{0,2},{1,3},{2,0},{3,1},{4,6},{5,7},{6,4},{7,5},{8,10},{9,11},{10,... | collective-permute-start | bytes 946184 | tf_op jit(solution)/shard_map/ppermute | solution.py:190
  57.0 8.7 %collective-permute-start.24 = (f32[616,128]{1,0:T(8,128)S(1)}, f32[616,128]{1,0:T(8,128)S(1)}, u32[]{:S(2)}, u32[]{:S(2)}) collective-permute-start(f32[616,128]{1,0:T(8,128)S(1)} %get-tuple-element.23), channel_id=1, source_target_pairs={{0,1},{1,0},{2,3},{3,2},{4,5},{5,4},{6,7},{7,6},{8,9},{9,8},{10,11... | collective-permute-start | bytes 946184 | tf_op jit(solution)/shard_map/ppermute | solution.py:190
  58.7 11.7 %collective-permute-start.4 = (f32[160,256]{1,0:T(8,128)S(1)}, f32[160,256]{1,0:T(8,128)S(1)}, u32[]{:S(2)}, u32[]{:S(2)}) collective-permute-start(f32[160,256]{1,0:T(8,128)S(1)} %collective-permute-done.2.refs_3_), channel_id=1, source_target_pairs={{0,8},{8,16},{16,24},{24,28},{28,20},{20,12},{12,4},{4,0},{1,9},{9... | collective-permute-start | bytes 491528 | tf_op jit(solution)/shard_map/ppermute | solution.py:158
  60.7 11.3 %collective-permute-start.5 = (f32[160,256]{1,0:T(8,128)S(1)}, f32[160,256]{1,0:T(8,128)S(1)}, u32[]{:S(2)}, u32[]{:S(2)}) collective-permute-start(f32[160,256]{1,0:T(8,128)S(1)} %collective-permute-done.3.refs_4_), channel_id=1, source_target_pairs={{8,0},{16,8},{24,16},{28,24},{20,28},{12,20},{4,12},{0,4},{9,1},{1... | collective-permute-start | bytes 491528 | tf_op jit(solution)/shard_map/ppermute | solution.py:159
  62.9 10.6 %collective-permute-start.35 = (f32[616,128]{1,0:T(8,128)S(1)}, f32[616,128]{1,0:T(8,128)S(1)}, u32[]{:S(2)}, u32[]{:S(2)}) collective-permute-start(f32[616,128]{1,0:T(8,128)S(1)} %get-tuple-element.27), channel_id=1, source_target_pairs={{0,1},{1,0},{2,3},{3,2},{4,5},{5,4},{6,7},{7,6},{8,9},{9,8},{10,11... | collective-permute-start | bytes 946184 | tf_op jit(solution)/shard_map/ppermute | solution.py:190
  63.5 10.3 %collective-permute-start.36 = (f32[616,128]{1,0:T(8,128)S(1)}, f32[616,128]{1,0:T(8,128)S(1)}, u32[]{:S(2)}, u32[]{:S(2)}) collective-permute-start(f32[616,128]{1,0:T(8,128)S(1)} %get-tuple-element.28), channel_id=1, source_target_pairs={{0,2},{1,3},{2,0},{3,1},{4,6},{5,7},{6,4},{7,5},{8,10},{9,11},{10,... | collective-permute-start | bytes 946184 | tf_op jit(solution)/shard_map/ppermute | solution.py:190
  67.9 11.4 %collective-permute-start.25 = (f32[616,128]{1,0:T(8,128)S(1)}, f32[616,128]{1,0:T(8,128)S(1)}, u32[]{:S(2)}, u32[]{:S(2)}) collective-permute-start(f32[616,128]{1,0:T(8,128)S(1)} %get-tuple-element.24), channel_id=1, source_target_pairs={{0,1},{1,0},{2,3},{3,2},{4,5},{5,4},{6,7},{7,6},{8,9},{9,8},{10,11... | collective-permute-start | bytes 946184 | tf_op jit(solution)/shard_map/ppermute | solution.py:190
  70.4 9.2 %collective-permute-start.26 = (f32[616,128]{1,0:T(8,128)S(1)}, f32[616,128]{1,0:T(8,128)S(1)}, u32[]{:S(2)}, u32[]{:S(2)}) collective-permute-start(f32[616,128]{1,0:T(8,128)S(1)} %get-tuple-element.25), channel_id=1, source_target_pairs={{0,2},{1,3},{2,0},{3,1},{4,6},{5,7},{6,4},{7,5},{8,10},{9,11},{10,... | collective-permute-start | bytes 946184 | tf_op jit(solution)/shard_map/ppermute | solution.py:190
  (8 other events, 36.4 us)
